TPU v7x, 128 devices: a whole 4x4x4 slice. The times are simulated.
128 devices in a mesh: row: 8 (over y, core), col: 16 (over x, z).
Axes of the slice: x: 4, y: 4, z: 4, core: 2. Of those that a mesh axis runs over, the one named last changes fastest.
Arguments:
- upper_a: bfloat16 [2, 4096, 8192], P(None, 'row', 'col'), may hold values from -0.125 to 0.125
- upper_b: bfloat16 [4, 4096, 2, 8192], P(None, 'row', None, 'col'), may hold values from -0.125 to 0.125
- right_side: bfloat16 [2, 4096, 2, 8192], P(None, 'row', None, 'col'), may hold values from -6 to 6
- a_bases: bfloat16 [2, 4096, 512], P(None, 'row'), may hold values from -1 to 1, as said below
- b_bases: bfloat16 [2, 8192, 512], P(None, 'col'), may hold values from -1 to 1, as said below
- a_values: float32 [2, 4096], P(None, 'row'), may hold values from 0.25 to 4
- b_values: float32 [2, 8192], P(None, 'col'), may hold values from 0.25 to 4
Outputs:
- solution: float32 [2, 4096, 2, 8192], P(None, 'row', None, 'col')
Inputs may be any that keep to these rules, and one draw needn't show every extreme that they name: Each tile of a_bases is an orthonormal matrix rounded to bfloat16. Each tile of b_bases is an orthonormal matrix rounded to bfloat16.
All inputs are finite; a program needn't handle non-finite values.
Results may differ from a plain program's by a relative error of at most 0.012.
Values may be sent and summed in bfloat16 or wider, within the bound.
A program may use at most 128 MiB of HBM per device.

v0:
```python
import jax
import jax.numpy as jnp
from jax import lax
from jax.sharding import PartitionSpec as P

FRONTS = 4


def passed_along(block, axis, distance):
    devices = range(lax.axis_size(axis))
    route = [((i - distance) % len(devices), i) for i in devices]
    return lax.ppermute(block, axis, route)


def broadcast(value, axis, root):
    return lax.dynamic_index_in_dim(lax.all_gather(value, axis), root, 0, keepdims=False)


def spread(block, axis, holder):
    block = jnp.where(lax.axis_index(axis) == holder, block, jnp.zeros_like(block))
    return lax.psum(block, axis)


def solve_tile(waiting, basis_left, values_left, basis_right, values_right):
    rounded = waiting.astype(jnp.bfloat16)
    first_half = lax.dot_general(
        basis_left, rounded, (((0,), (0,)), ((), ())), preferred_element_type=jnp.float32
    ).astype(jnp.bfloat16)
    scaled = jnp.dot(first_half, basis_right, preferred_element_type=jnp.float32)
    scaled = (scaled / (values_left[:, None] + values_right[None, :])).astype(jnp.bfloat16)
    left_side = jnp.dot(basis_left, scaled, preferred_element_type=jnp.float32).astype(jnp.bfloat16)
    return lax.dot_general(
        left_side, basis_right, (((1,), (1,)), ((), ())), preferred_element_type=jnp.float32
    ).astype(jnp.bfloat16)


def skip_tile(waiting, basis_left, values_left, basis_right, values_right):
    return jnp.zeros(waiting.shape, jnp.bfloat16)


def shift_columns(block, offset):
    return passed_along(block, "col", offset)


def shift_used(block, offset):
    return passed_along(block, "row", offset)


def shards(upper_a, upper_b, right_side, a_bases, b_bases, a_values, b_values):
    row_count = lax.axis_size("row")
    col_count = lax.axis_size("col")
    row_id = lax.axis_index("row")
    col_id = lax.axis_index("col")
    tile_rows = right_side.shape[0]
    tile_cols = right_side.shape[2]
    b_local_rows = upper_b.shape[0]
    first_front = col_count - 2
    rows_glob = jnp.arange(tile_rows, dtype=jnp.int32) * row_count + row_id
    cols_glob = jnp.arange(tile_cols, dtype=jnp.int32) * col_count + col_id
    working = right_side.astype(jnp.float32)
    a_blocks = []
    for front_step in range(FRONTS):
        if front_step == 1:
            a_blocks.append(upper_a)
        else:
            a_blocks.append(shift_columns(upper_a, front_step - 1))
    b_blocks = []
    for front_step in range(FRONTS):
        target_row = (row_id + 1 - front_step) % row_count
        target_glob = jnp.arange(tile_rows, dtype=jnp.int32) * row_count + target_row
        picks = jnp.clip((front_step - 1 + target_glob) // row_count, 0, b_local_rows - 1)
        chosen = jnp.take(upper_b, picks, axis=0)
        if front_step == 1:
            b_blocks.append(chosen)
        else:
            b_blocks.append(shift_used(chosen, 1 - front_step))
    front_of = (col_count - 1 - rows_glob)[:, None] + cols_glob[None, :]
    for front_step in range(FRONTS):
        front_id = first_front + front_step
        owned = front_of == front_id
        holder = jnp.any(owned)
        flat_index = jnp.argmax(owned.reshape(-1).astype(jnp.int32))
        a_pick = flat_index // tile_cols
        b_pick = flat_index % tile_cols
        waiting = working[a_pick, :, b_pick, :]
        x_tile = lax.cond(
            holder,
            solve_tile,
            skip_tile,
            waiting,
            a_bases[a_pick],
            a_values[a_pick],
            b_bases[b_pick],
            b_values[b_pick],
        )
        working = working.at[a_pick, :, b_pick, :].set(
            jnp.where(holder, x_tile.astype(jnp.float32), waiting)
        )
        column_x = broadcast(x_tile, "row", (1 - front_step + col_id) % row_count)
        row_list = []
        for row_part in range(tile_rows):
            root_col = (front_step - 1 + row_part * row_count + row_id) % col_count
            row_list.append(spread(x_tile, "col", root_col))
        row_x = jnp.stack(row_list)
        k_glob = col_count - 1 - front_id + cols_glob
        k_valid = (k_glob >= 0) & (k_glob <= col_count - 1)
        column_mask = (k_valid[None, :] & (rows_glob[:, None] < k_glob[None, :])).astype(
            jnp.float32
        )
        column_terms = jnp.einsum(
            "apq,qr->apr", a_blocks[front_step], column_x, preferred_element_type=jnp.float32
        )
        l_glob = front_id - col_count + 1 + rows_glob
        row_mask = ((l_glob[:, None] >= 0) & (l_glob[:, None] < cols_glob[None, :])).astype(
            jnp.float32
        )
        row_terms = jnp.einsum(
            "apq,aqbr->apbr", row_x, b_blocks[front_step], preferred_element_type=jnp.float32
        )
        working = (
            working
            - column_terms[:, :, None, :] * column_mask[:, None, :, None]
            - row_terms * row_mask[:, None, :, None]
        )
    return working


def solution(mesh):
    return jax.shard_map(
        shards,
        mesh=mesh,
        in_specs=(
            P(None, "row", "col"),
            P(None, "row", None, "col"),
            P(None, "row", None, "col"),
            P(None, "row", None),
            P(None, "col", None),
            P(None, "row"),
            P(None, "col"),
        ),
        out_specs=P(None, "row", None, "col"),
        check_vma=False,
    )
```

profile of v0, /device:TPU:76, one launch (start us, length us, event | category | flops | bytes accessed | tf_op | source)
XLA Modules:
  0.0 489.7 jit_solution(4523634216439111667)
XLA Ops:
  7.5 0.8 and_convert_fusion.1
  11.5 4.3 copy_convert_fusion
  16.5 2.3 dynamic-slice_bitcast_fusion.3
  18.9 0.8 copy-done.2
  19.8 7.0 %gather_fusion = bf16[2,512,2,512]{3,2,1,0:T(2,128)(2,1)S(1)} fusion(bf16[4,512,2,512]{3,2,1,0:T(2,128)(2,1)} %param.26, s32[1024]{0:T(1024)S(1)} %pad_clamp_fusion.3), kind=kCustom, calls=%fused_computation.clone | custom fusion | bytes 4194312 | tf_op jit(solution)/shard_map/jit(_take)/gather | solution.py:72
  26.9 1.7 copy_select_fusion.2
  28.6 3.7 collective-permute-start.1
  32.5 1.1 select_bitcast_fusion.7
  37.6 0.7 and_reduce_fusion.2
  38.3 4.0 fusion.88
  42.3 19.7 %collective-permute-done = bf16[2,512,512]{2,1,0:T(8,128)(2,1)S(1)} collective-permute-done((bf16[2,512,512]{2,1,0:T(8,128)(2,1)}, bf16[2,512,512]{2,1,0:T(8,128)(2,1)S(1)}, u32[]{:S(2)}, u32[]{:S(2)}) %collective-permute-start) | collective-permute-done | bytes 1048608 | tf_op jit(solution)/shard_map/ppermute | solution.py:12
  61.9 1.7 all-gather.9.cloned.1.call-done
  63.6 3.2 convolution_bitcast_fusion.3
  66.8 1.9 copy.21
  68.7 59.7 %all-reduce.15.cloned.1.call-done = (bf16[1,512,512]{2,1,0:T(8,128)(2,1)}, bf16[1,512,512]{2,1,0:T(8,128)(2,1)}) async-done(((bf16[1,512,512]{2,1,0:T(8,128)(2,1)}, bf16[1,512,512]{2,1,0:T(8,128)(2,1)}), (bf16[1,512,512]{2,1,0:T(8,128)(2,1)}, bf16[1,512,512]{2,1,0:T(8,128)(2,1)})) %all-reduce.15.cloned.1.call-update) | async-done | bytes 1048592 | tf_op jit(solution)/shard_map/psum | solution.py:21
  128.4 6.5 %multiply_subtract_fusion.3 = f32[2,512,2,512]{3,1,2,0:T(8,128)} fusion(f32[2,512,2,512]{3,1,2,0:T(8,128)} %fusion.88, bf16[2,512,2,512]{3,1,2,0:T(8,128)(2,1)} %collective-permute-done.1, f32[2,2]{1,0:T(2,128)S(1)} %get-tuple-element.403, f32[2,2]{1,0:T(2,128)S(1)} %get-tuple-element.390, f32[2,512,512]{2,1,0:T(8,128)S(1)} %copy.21, ...), kind=kOutput, calls=%fused_computation.79 | convolution fusion | flops 1080033280 | bytes 13631520 | tf_op jit(solution)/shard_map/apq,aqbr->apbr/dot_general | solution.py:117
  135.0 2.4 dynamic-slice_bitcast_fusion.2
  137.4 2.7 conditional.5
  137.4 2.0 fusion.19
  139.4 0.7 convolution_convert_fusion.3
  140.1 0.8 copy-done.4
  144.5 8.0 %gather_fusion.1 = bf16[2,512,2,512]{3,2,1,0:T(2,128)(2,1)} fusion(bf16[4,512,2,512]{3,2,1,0:T(2,128)(2,1)} %param.26, s32[1024]{0:T(1024)S(1)} %pad_clamp_fusion.2), kind=kCustom, calls=%fused_computation.1.clone | custom fusion | bytes 4194312 | tf_op jit(solution)/shard_map/jit(_take)/gather | solution.py:72
  153.0 1.1 select_bitcast_fusion.5
  154.2 3.5 broadcast_select_fusion
  157.6 3.7 fusion.87
  161.4 11.5 %all-gather.11.cloned.1.call-done = bf16[4096,512]{1,0:T(8,128)(2,1)} async-done(((bf16[512,512]{1,0:T(8,128)(2,1)}), bf16[4096,512]{1,0:T(8,128)(2,1)}) %all-gather.11.cloned.1.call-update) | async-done | bytes 4194320 | tf_op jit(solution)/shard_map/all_gather | solution.py:16
  172.9 3.5 convolution_bitcast_fusion.2
  176.4 2.9 copy.24
  179.3 60.6 %all-reduce.13.cloned.1.call-done = (bf16[1,512,512]{2,1,0:T(8,128)(2,1)}, bf16[1,512,512]{2,1,0:T(8,128)(2,1)}) async-done(((bf16[1,512,512]{2,1,0:T(8,128)(2,1)}, bf16[1,512,512]{2,1,0:T(8,128)(2,1)}), (bf16[1,512,512]{2,1,0:T(8,128)(2,1)}, bf16[1,512,512]{2,1,0:T(8,128)(2,1)})) %all-reduce.13.cloned.1.call-update) | async-done | bytes 1048592 | tf_op jit(solution)/shard_map/psum | solution.py:21
  239.9 4.6 multiply_subtract_fusion.2
  244.6 2.0 copy-done
  246.6 1.1 dynamic-slice_bitcast_fusion.1
  248.2 0.8 copy-done.6
  249.2 7.0 %gather_fusion.2 = bf16[2,512,2,512]{3,2,1,0:T(2,128)(2,1)S(1)} fusion(bf16[4,512,2,512]{3,2,1,0:T(2,128)(2,1)} %param.26, s32[1024]{0:T(1024)S(1)} %pad_clamp_fusion.1), kind=kCustom, calls=%fused_computation.2.clone | custom fusion | bytes 4194312 | tf_op jit(solution)/shard_map/jit(_take)/gather | solution.py:72
  256.2 1.7 copy_select_fusion.1
  258.0 1.9 collective-permute-start.3
  259.9 3.1 collective-permute-start.2
  263.0 1.1 select_bitcast_fusion.3
  268.3 0.7 and_reduce_fusion
  269.0 4.0 fusion.86
  273.0 17.7 %collective-permute-done.2 = bf16[2,512,512]{2,1,0:T(8,128)(2,1)S(1)} collective-permute-done((bf16[2,512,512]{2,1,0:T(8,128)(2,1)}, bf16[2,512,512]{2,1,0:T(8,128)(2,1)S(1)}, u32[]{:S(2)}, u32[]{:S(2)}) %collective-permute-start.2) | collective-permute-done | bytes 1048608 | tf_op jit(solution)/shard_map/ppermute | solution.py:12
  290.7 2.2 all-gather.13.cloned.1.call-done
  292.9 3.2 convolution_bitcast_fusion.1
  296.1 1.9 copy.27
  298.0 2.7 collective-permute-done.3
  300.6 55.7 %all-reduce.11.cloned.1.call-done = (bf16[1,512,512]{2,1,0:T(8,128)(2,1)}, bf16[1,512,512]{2,1,0:T(8,128)(2,1)}) async-done(((bf16[1,512,512]{2,1,0:T(8,128)(2,1)}, bf16[1,512,512]{2,1,0:T(8,128)(2,1)}), (bf16[1,512,512]{2,1,0:T(8,128)(2,1)}, bf16[1,512,512]{2,1,0:T(8,128)(2,1)})) %all-reduce.11.cloned.1.call-update) | async-done | bytes 1048592 | tf_op jit(solution)/shard_map/psum | solution.py:21
  356.3 4.5 multiply_subtract_fusion.1
  360.9 2.0 copy-done.1
  362.9 1.1 dynamic-slice_bitcast_fusion
  364.9 0.8 copy-done.8
  365.7 7.0 %gather_fusion.3 = bf16[2,512,2,512]{3,2,1,0:T(2,128)(2,1)S(1)} fusion(bf16[4,512,2,512]{3,2,1,0:T(2,128)(2,1)} %param.26, s32[1024]{0:T(1024)S(1)} %pad_clamp_fusion), kind=kCustom, calls=%fused_computation.3.clone | custom fusion | bytes 4194312 | tf_op jit(solution)/shard_map/jit(_take)/gather | solution.py:72
  372.8 1.7 copy_select_fusion
  374.5 3.2 collective-permute-start.5
  377.7 2.2 collective-permute-start.4
  379.9 1.1 select_bitcast_fusion.1
  381.0 4.0 fusion.85
  385.1 18.1 %collective-permute-done.4 = bf16[2,512,512]{2,1,0:T(8,128)(2,1)S(1)} collective-permute-done((bf16[2,512,512]{2,1,0:T(8,128)(2,1)}, bf16[2,512,512]{2,1,0:T(8,128)(2,1)S(1)}, u32[]{:S(2)}, u32[]{:S(2)}) %collective-permute-start.4) | collective-permute-done | bytes 1048608 | tf_op jit(solution)/shard_map/ppermute | solution.py:12
  403.2 14.3 %all-gather.15.cloned.1.call-done = bf16[4096,512]{1,0:T(8,128)(2,1)} async-done(((bf16[512,512]{1,0:T(8,128)(2,1)}), bf16[4096,512]{1,0:T(8,128)(2,1)}) %all-gather.15.cloned.1.call-update) | async-done | bytes 4194320 | tf_op jit(solution)/shard_map/all_gather | solution.py:16
  417.5 3.2 convolution_bitcast_fusion
  420.7 1.9 copy.30
  422.6 14.6 %collective-permute-done.5 = bf16[2,512,2,512]{3,1,2,0:T(8,128)(2,1)} collective-permute-done((bf16[2,512,2,512]{3,1,2,0:T(8,128)(2,1)}, bf16[2,512,2,512]{3,1,2,0:T(8,128)(2,1)}, u32[]{:S(2)}, u32[]{:S(2)}) %collective-permute-start.5) | collective-permute-done | bytes 2097184 | tf_op jit(solution)/shard_map/ppermute | solution.py:12
  437.2 35.4 %all-reduce.9.cloned.1.call-done = (bf16[1,512,512]{2,1,0:T(8,128)(2,1)}, bf16[1,512,512]{2,1,0:T(8,128)(2,1)}) async-done(((bf16[1,512,512]{2,1,0:T(8,128)(2,1)}, bf16[1,512,512]{2,1,0:T(8,128)(2,1)}), (bf16[1,512,512]{2,1,0:T(8,128)(2,1)}, bf16[1,512,512]{2,1,0:T(8,128)(2,1)})) %all-reduce.9.cloned.1.call-update) | async-done | bytes 1048592 | tf_op jit(solution)/shard_map/psum | solution.py:21
  472.6 4.5 multiply_subtract_fusion
  477.1 5.2 %copy.32 = f32[2,512,2,512]{3,2,1,0:T(2,128)} copy(f32[2,512,2,512]{3,1,2,0:T(8,128)S(1)} %multiply_subtract_fusion) | data formatting | bytes 8388608 | tf_op jit(solution)/shard_map/sub | solution.py:121
  (83 shorter events, 5.9 us)
Async XLA Ops:
  7.4 56.3 %all-gather.9.cloned.1.call-start = ((), (), s32[]{:S(2)}) async-start(), calls=%async_computation | async-start | bytes 4718592 | tf_op jit(solution)/shard_map/all_gather | solution.py:16
  15.8 3.0 copy-start.10
  15.8 3.0 copy-start.11
  15.8 3.0 copy-start.13
  18.9 0.8 copy-start.2
  19.7 108.7 %all-reduce.15.cloned.1.call-start = ((), (), s32[]{:S(2)}) async-start(), calls=%async_computation.7 | async-start | bytes 2097152 | tf_op jit(solution)/shard_map/psum | solution.py:21
  26.8 5.7 %copy-start.3 = (bf16[512,512]{1,0:T(8,128)(2,1)S(1)}, bf16[512,512]{1,0:T(8,128)(2,1)}, u32[]{:S(2)}) copy-start(bf16[512,512]{1,0:T(8,128)(2,1)} %copy-done.2) | copy-start | bytes 1572868
  28.6 9.0 %copy-start.12 = (s32[4]{0:T(128)S(1)}, s32[4]{0:T(128)}, u32[]{:S(2)}) copy-start(s32[4]{0:T(128)} %constant.378.clone.1) | copy-start | bytes 52
  28.6 99.9 %collective-permute-start.1 = (bf16[2,512,2,512]{3,1,2,0:T(8,128)(2,1)}, bf16[2,512,2,512]{3,1,2,0:T(8,128)(2,1)}, u32[]{:S(2)}, u32[]{:S(2)}) collective-permute-start(bf16[2,512,2,512]{3,1,2,0:T(8,128)(2,1)} %copy_select_fusion.2), channel_id=1, source_target_pairs={{112,0},{0,16},{16,32},{32,48},{48,64},{64,80},{80,96},{96,112},{1... | collective-permute-start | bytes 6291464 | tf_op jit(solution)/shard_map/ppermute | solution.py:12
  32.3 29.7 %collective-permute-start = (bf16[2,512,512]{2,1,0:T(8,128)(2,1)}, bf16[2,512,512]{2,1,0:T(8,128)(2,1)S(1)}, u32[]{:S(2)}, u32[]{:S(2)}) collective-permute-start(bf16[2,512,512]{2,1,0:T(8,128)(2,1)} %param.25), channel_id=1, source_target_pairs={{1,0},{2,1},{3,2},{4,3},{5,4},{6,5},{7,6},{8,7},{9,8},{10,9},{11,1... | collective-permute-start | bytes 3145736 | tf_op jit(solution)/shard_map/ppermute | solution.py:12
  33.6 139.3 %all-gather.11.cloned.1.call-start = ((), (), s32[]{:S(2)}) async-start(), calls=%async_computation.1 | async-start | bytes 4718592 | tf_op jit(solution)/shard_map/all_gather | solution.py:16
  135.0 2.4 copy-start.14
  135.0 2.4 copy-start.17
  140.1 0.8 copy-start.4
  140.9 99.0 %all-reduce.13.cloned.1.call-start = ((), (), s32[]{:S(2)}) async-start(), calls=%async_computation.6 | async-start | bytes 2097152 | tf_op jit(solution)/shard_map/psum | solution.py:21
  144.5 8.6 %copy-start.5 = (bf16[512,512]{1,0:T(8,128)(2,1)S(1)}, bf16[512,512]{1,0:T(8,128)(2,1)}, u32[]{:S(2)}) copy-start(bf16[512,512]{1,0:T(8,128)(2,1)} %copy-done.4) | copy-start | bytes 1572868
  154.1 138.8 %all-gather.13.cloned.1.call-start = ((), (), s32[]{:S(2)}) async-start(), calls=%async_computation.2 | async-start | bytes 4718592 | tf_op jit(solution)/shard_map/all_gather | solution.py:16
  244.5 2.0 copy-start
  246.6 1.6 copy-start.15
  248.2 0.8 copy-start.6
  249.0 107.3 %all-reduce.11.cloned.1.call-start = ((), (), s32[]{:S(2)}) async-start(), calls=%async_computation.5 | async-start | bytes 2097152 | tf_op jit(solution)/shard_map/psum | solution.py:21
  256.2 6.8 %copy-start.7 = (bf16[512,512]{1,0:T(8,128)(2,1)S(1)}, bf16[512,512]{1,0:T(8,128)(2,1)}, u32[]{:S(2)}) copy-start(bf16[512,512]{1,0:T(8,128)(2,1)} %copy-done.6) | copy-start | bytes 1572868
  258.0 42.7 %collective-permute-start.3 = (bf16[2,512,2,512]{3,1,2,0:T(8,128)(2,1)}, bf16[2,512,2,512]{3,1,2,0:T(8,128)(2,1)}, u32[]{:S(2)}, u32[]{:S(2)}) collective-permute-start(bf16[2,512,2,512]{3,1,2,0:T(8,128)(2,1)} %copy_select_fusion.1), channel_id=1, source_target_pairs={{16,0},{32,16},{48,32},{64,48},{80,64},{96,80},{112,96},{0,112},{1... | collective-permute-start | bytes 6291464 | tf_op jit(solution)/shard_map/ppermute | solution.py:12
  259.9 30.8 %collective-permute-start.2 = (bf16[2,512,512]{2,1,0:T(8,128)(2,1)}, bf16[2,512,512]{2,1,0:T(8,128)(2,1)S(1)}, u32[]{:S(2)}, u32[]{:S(2)}) collective-permute-start(bf16[2,512,512]{2,1,0:T(8,128)(2,1)} %param.25), channel_id=1, source_target_pairs={{15,0},{0,1},{1,2},{2,3},{3,4},{4,5},{5,6},{6,7},{7,8},{8,9},{9,10... | collective-permute-start | bytes 3145736 | tf_op jit(solution)/shard_map/ppermute | solution.py:12
  264.1 153.4 %all-gather.15.cloned.1.call-start = ((), (), s32[]{:S(2)}) async-start(), calls=%async_computation.3 | async-start | bytes 4718592 | tf_op jit(solution)/shard_map/all_gather | solution.py:16
  360.9 2.0 copy-start.1
  362.9 1.6 copy-start.16
  362.9 1.9 copy-start.18
  364.8 0.8 copy-start.8
  365.7 106.9 %all-reduce.9.cloned.1.call-start = ((), (), s32[]{:S(2)}) async-start(), calls=%async_computation.4 | async-start | bytes 2097152 | tf_op jit(solution)/shard_map/psum | solution.py:21
  372.8 7.2 %copy-start.9 = (bf16[512,512]{1,0:T(8,128)(2,1)S(1)}, bf16[512,512]{1,0:T(8,128)(2,1)}, u32[]{:S(2)}) copy-start(bf16[512,512]{1,0:T(8,128)(2,1)} %copy-done.8) | copy-start | bytes 1572868
  374.5 62.7 %collective-permute-start.5 = (bf16[2,512,2,512]{3,1,2,0:T(8,128)(2,1)}, bf16[2,512,2,512]{3,1,2,0:T(8,128)(2,1)}, u32[]{:S(2)}, u32[]{:S(2)}) collective-permute-start(bf16[2,512,2,512]{3,1,2,0:T(8,128)(2,1)} %copy_select_fusion), channel_id=1, source_target_pairs={{32,0},{48,16},{64,32},{80,48},{96,64},{112,80},{0,96},{16,112},{3... | collective-permute-start | bytes 6291464 | tf_op jit(solution)/shard_map/ppermute | solution.py:12
  377.7 25.5 %collective-permute-start.4 = (bf16[2,512,512]{2,1,0:T(8,128)(2,1)}, bf16[2,512,512]{2,1,0:T(8,128)(2,1)S(1)}, u32[]{:S(2)}, u32[]{:S(2)}) collective-permute-start(bf16[2,512,512]{2,1,0:T(8,128)(2,1)} %param.25), channel_id=1, source_target_pairs={{14,0},{15,1},{0,2},{1,3},{2,4},{3,5},{4,6},{5,7},{6,8},{7,9},{8,1... | collective-permute-start | bytes 3145736 | tf_op jit(solution)/shard_map/ppermute | solution.py:12
Sparse Core Ops, SparseCore 0:
  19.8 43.7 all-gather.8
  141.0 31.7 all-gather.10
  249.1 43.7 all-gather.12
  365.8 51.6 all-gather.14
Sparse Core Ops, SparseCore 1:
  33.7 94.7 all-reduce.14
  154.2 85.7 all-reduce.12
  264.2 92.1 all-reduce.10
  381.1 91.4 all-reduce.8
where the time goes:
time: 494 us; the launch traced here: 490 us
  waiting for transfers between devices  314 us (64%)
  local copies, waits for them, and re-layouts  58.9 us (12%)
  other arithmetic  38 us (8%)
  matrix products  35.8 us (7%)
  between operations  27.8 us (6%)
  starting transfers between devices  15.2 us (3%)
    psum x4, waiting for transfers between devices, spread(): return lax.psum(block, axis)  211 us
    ppermute x6, waiting for transfers between devices, passed_along(): return lax.ppermute(block, axis, route)  72.7 us
    all_gather x4, waiting for transfers between devices, broadcast(): lax.all_gather(value, axis)  29.8 us
    gather x4, local copies, waits for them, and re-layouts, shards(): chosen = jnp.take(upper_b, picks, axis=0)  29.1 us
    dot_general x4, matrix products, shards(): jnp.einsum('apq,aqbr->apbr', row_x, b_blocks[front_step], preferred_eleme...  20.2 us
    scatter x4, other arithmetic, shards(): working.at[a_pick, :, b_pick, :]  15.7 us
    ppermute x6, starting transfers between devices, passed_along(): return lax.ppermute(block, axis, route)  14.5 us
    dot_general x4, matrix products, shards(): jnp.einsum('apq,qr->apr', a_blocks[front_step], column_x, preferred_eleme...  13 us
  transfers between devices with their start and end apart: 14, of which 13 were waited for; matrix products, arithmetic and copies ran while one was open for 17% of the time, Pallas kernels for 0%

commit v1 on v0

v1 whole, which is shorter than its diff:
```python
import functools

import jax
import jax.numpy as jnp
from jax import lax
from jax.experimental import pallas as pl
from jax.experimental.pallas import tpu as pltpu
from jax.sharding import PartitionSpec as P

MESH = pl.DeviceIdType.MESH
FRONTS = 4
RING = 4
PIECES = 2


def plan(nb, n_row, n_col, a_in, b_in, c_in, qa_in, qb_in, av_in, bv_in, out,
         a_buf, b_buf, xc, xr, w, c_buf, qa, qat, qb, inv, half, av, bv,
         local_sem, out_sem, a_send, b_send, a_recv, b_recv, xc_send, xr_send, xc_recv, xr_recv):
    rows = nb // PIECES
    r = lax.axis_index("row")
    c = lax.axis_index("col")
    y, core = r // 2, r % 2
    x, z = c // RING, c % RING
    mod = lax.rem

    def row_of(yy, kk):
        return mod(yy + 2 * RING, RING) * 2 + kk

    def col_of(xx, zz):
        return mod(xx + 2 * RING, RING) * RING + mod(zz + 2 * RING, RING)

    col_next = mod(c + 1, n_col)
    col_prev = mod(c + n_col - 1, n_col)

    shift = mod(c - r + 1 + n_col, n_col)
    turn = mod(shift, 8)
    a_own = shift // 8
    l_own = r + 8 * a_own - 1 + turn
    b_own = jnp.where(l_own >= n_col, 1, 0)
    solves = (turn < FRONTS) & (l_own >= 0)
    turn = jnp.where(solves, turn, 99)

    def remote(src, dst, send, recv, row, col):
        return pltpu.make_async_remote_copy(
            src_ref=src, dst_ref=dst, send_sem=send, recv_sem=recv,
            device_id=(row, col), device_id_type=MESH)

    def k_of(s, col):
        return mod(col + 1 - s + n_col, n_col)

    def has_col(s, col):
        return jnp.logical_not((s == 0) & (col == n_col - 1))

    def needs_a(s, row, col, a):
        return has_col(s, col) & (row + 8 * a < k_of(s, col))

    def needs_b(s, row, col, a, b):
        l = row + 8 * a - 1 + s
        return (l >= 0) & (l < col + n_col * b)

    def a_copy(s, a, col, src):
        return remote(src, a_buf.at[s, a], a_send.at[s, a], a_recv.at[s, a], r, col)

    def b_copy(s, a, b, row, src):
        return remote(src, b_buf.at[s, a, b], b_send.at[s, a, b], b_recv.at[s, a, b], row, c)

    def hand_b(a, b):
        return remote(b_buf.at[2, a, b], b_buf.at[3, a, b], b_send.at[1, a, b], b_recv.at[3, a, b], partner, c)

    def each_a(fn):
        for a in range(2):
            fn(a)

    def each_ab(fn):
        for a in range(2):
            for b in range(2):
                fn(a, b)

    def send_a(s, col):
        def one(a):
            @pl.when(needs_a(s, r, col, a))
            def _():
                a_copy(s, a, col, a_in.at[a]).start()
        each_a(one)

    def send_b(s, row):
        def one(a, b):
            @pl.when(needs_b(s, row, c, a, b))
            def _():
                l4 = (row + 8 * a - 1 + s) // 8
                b_copy(s, a, b, row, b_in.at[l4, b]).start()
        each_ab(one)

    row_next = mod(r + 1, n_row)
    row_prev = mod(r + n_row - 1, n_row)
    row_prev2 = mod(r + n_row - 2, n_row)
    partner = y * 2 + 1 - core

    def col_route(s, q):
        g = 1 if q % 2 == 0 else -1
        k = k_of(s, c)
        rr = mod(k, 8)
        ry = rr // 2
        valid = has_col(s, c)
        root = valid & (r == rr)
        oy = mod((y - ry) * g + RING, RING)
        relay = valid & (oy != 0) & (core == 1)
        piece = pl.ds(q * rows, rows)

        def copy(n, row):
            return remote(xc.at[s, piece], xc.at[s, piece], xc_send.at[s, q, n], xc_recv.at[s, q], row, c)

        sends = [
            (root | (relay & (oy == 1)), copy(0, row_of(y + g, 1))),
            (root, copy(1, row_of(y - g, 1))),
            (root | relay, copy(2, partner)),
        ]
        return valid & (r != rr), sends, copy(2, partner)

    def row_route(s, a, q):
        g = 1 if q % 2 == 0 else -1
        l = r + 8 * a - 1 + s
        valid = l >= 0
        lc = mod(l + n_col, n_col)
        rx, rz = lc // RING, lc % RING
        root = valid & (c == lc)
        oz = mod((z - rz) * g + RING, RING)
        ox = mod((x - rx) * g + RING, RING)
        early = (rz == RING - 1) & (z == 0) & (ox == 0)
        forth = valid & ((ox == 0) | (ox == 1))
        back = valid & (ox == 0)
        if g == 1:
            forth = forth & jnp.logical_not(early)
        else:
            back = back & jnp.logical_not(early)
        piece = pl.ds(q * rows, rows)

        def copy(n, col):
            return remote(xr.at[s, a, piece], xr.at[s, a, piece], xr_send.at[s, a, q, n], xr_recv.at[s, a, q], r, col)

        sends = [
            (valid & (ox == 0) & ((oz == 0) | (oz == 1)), copy(0, col_of(x, z + g))),
            (root & (rz == RING - 1), copy(4, col_next)),
            (valid & (ox == 0) & (oz == 0), copy(1, col_of(x, z - g))),
            (forth, copy(2, col_of(x + g, z))),
            (back, copy(3, col_of(x - g, z))),
        ]
        return valid & (c != lc), sends, copy(0, col_of(x, z + g))

    def launch(sends):
        for when, copy in sends:
            @pl.when(when)
            def _(copy=copy):
                copy.start()

    def collect(sends):
        for when, copy in sends:
            @pl.when(when)
            def _(copy=copy):
                copy.wait_send()

    def take_col(s):
        for q in range(PIECES):
            arrives, sends, copy = col_route(s, q)

            @pl.when(arrives)
            def _():
                copy.wait_recv()
                launch(sends)

    def take_row(s, a):
        for q in range(PIECES):
            arrives, sends, copy = row_route(s, a, q)

            @pl.when(arrives)
            def _():
                copy.wait_recv()
                launch(sends)

    f32 = jnp.float32

    def matmul(p, q):
        return jnp.dot(p, q, preferred_element_type=f32)

    def update(s, a, b):
        i, j = r + 8 * a, c + n_col * b
        k = j + 1 - s

        @pl.when((k >= 0) & (k < n_col) & (i < k))
        def _():
            @pl.when(s != 2)
            def _():
                a_copy(s, a, c, a_buf.at[s, a]).wait_recv()
            w[a, b] = w[a, b] - matmul(a_buf[s, a], xc[s])

        @pl.when(needs_b(s, r, c, a, b))
        def _():
            @pl.when(s != 2)
            def _():
                b_copy(s, a, b, r, b_buf.at[s, a, b]).wait_recv()
            w[a, b] = w[a, b] - matmul(xr[s, a], b_buf[s, a, b])

    def solve(s):
        half[0] = w[a_own, b_own].astype(jnp.bfloat16)
        half[1] = matmul(qat[...], half[0]).astype(jnp.bfloat16)
        half[0] = (matmul(half[1], qb[...]) * inv[...]).astype(jnp.bfloat16)
        for q in range(PIECES):
            piece = pl.ds(q * rows, rows)
            left = matmul(qa[piece, :], half[0]).astype(jnp.bfloat16)
            tile = lax.dot_general(left, qb[...], (((1,), (1,)), ((), ())), preferred_element_type=f32)
            tile = tile.astype(jnp.bfloat16)
            xr[s, a_own, piece, :] = tile
            xc[s, piece, :] = tile
            w[a_own, b_own, piece, :] = tile.astype(f32)
            _, sends, _ = col_route(s, q)
            launch(sends)
            _, sends, _ = row_route(s, a_own, q)
            launch(sends)

    barrier = pltpu.get_barrier_semaphore()
    friends = [(partner, c), (r, col_next), (r, col_prev)]
    for d in (1, -1):
        friends += [(row_of(y + d, 0), c), (row_of(y + d, 1), c), (r, col_of(x, z + d)), (r, col_of(x + d, z))]
    for friend in friends:
        pl.semaphore_signal(barrier, inc=1, device_id=friend, device_id_type=MESH)

    loads = [
        pltpu.make_async_copy(c_in, c_buf, local_sem.at[0]),
        pltpu.make_async_copy(qa_in.at[a_own], qa, local_sem.at[1]),
        pltpu.make_async_copy(qb_in.at[b_own], qb, local_sem.at[2]),
        pltpu.make_async_copy(av_in.at[a_own], av, local_sem.at[3]),
        pltpu.make_async_copy(bv_in.at[b_own], bv, local_sem.at[4]),
    ]
    for load in loads:
        load.start()

    def local_a(a):
        return pltpu.make_async_copy(a_in.at[a], a_buf.at[1, a], a_recv.at[1, a])

    def local_b(a, b):
        return pltpu.make_async_copy(b_in.at[a, b], b_buf.at[1, a, b], b_recv.at[1, a, b])

    each_a(lambda a: pl.when(needs_a(1, r, c, a))(lambda: local_a(a).start()))
    each_ab(lambda a, b: pl.when(needs_b(1, r, c, a, b))(lambda: local_b(a, b).start()))

    pl.semaphore_wait(barrier, len(friends))
    send_a(0, col_prev)
    send_b(0, row_next)

    for load in loads:
        load.wait()

    @pl.when(solves)
    def _():
        qat[...] = qa[...].T
        down = jnp.broadcast_to(av[...], (128, nb)).T
        for n in range(nb // 128):
            lanes = pl.ds(n * 128, 128)
            inv[:, lanes] = 1.0 / (down + bv[:, lanes])

    def load_w(t, carry):
        w[t // 2, t % 2] = c_buf[t // 2, t % 2].astype(f32)
        return carry
    lax.fori_loop(0, 4, load_w, 0)

    def front(t, carry):
        s = t - 1

        @pl.when(t > 0)
        def _():
            take_col(s)
            take_row(s, jnp.where(solves, a_own, a_near(s)))

        ahead = turn == t

        @pl.when(ahead)
        def _():
            @pl.when(t > 0)
            def _():
                update(s, a_own, b_own)
            solve(t)

        @pl.when(t == 1)
        def _():
            send_a(2, col_next)
            send_b(2, row_prev)

        @pl.when(t > 0)
        def _():
            take_row(s, 1 - jnp.where(solves, a_own, a_near(s)))

            def rest(n, carry):
                a, b = n // 2, n % 2

                @pl.when(jnp.logical_not(ahead & (a == a_own) & (b == b_own)))
                def _():
                    update(s, a, b)

                @pl.when(t == FRONTS)
                def _():
                    pltpu.make_async_copy(w.at[a, b], out.at[a, b], out_sem.at[a, b]).start()
                return carry
            lax.fori_loop(0, 4, rest, 0)

        @pl.when(t == 2)
        def _():
            relay_two()
        return carry

    def a_near(s):
        l = mod(r - 1 + s + n_col, n_col)
        gap = mod(x - l // RING + RING, RING)
        return jnp.where((gap == 0) | (gap == 1), 0, 1)

    def relay_two():
        def one(a):
            @pl.when(needs_a(2, r, c, a))
            def _():
                a_copy(2, a, c, a_buf.at[2, a]).wait_recv()

            @pl.when(needs_a(3, r, col_next, a))
            def _():
                a_copy(3, a, col_next, a_buf.at[2, a]).start()
        each_a(one)

        @pl.when(core == 1)
        def _():
            send_b(3, row_prev2)

        def pair(a, b):
            @pl.when(needs_b(2, r, c, a, b))
            def _():
                b_copy(2, a, b, r, b_buf.at[2, a, b]).wait_recv()

                @pl.when(core == 1)
                def _():
                    hand_b(a, b).start()
        each_ab(pair)

    lax.fori_loop(0, FRONTS + 1, front, 0)

    def drain_a(a):
        for s, col in ((0, col_prev), (2, col_next), (3, col_next)):
            @pl.when(needs_a(s, r, col, a))
            def _(s=s, col=col):
                a_copy(s, a, col, a_in.at[a]).wait_send()
    each_a(drain_a)

    def drain_b(a, b):
        for s, row in ((0, row_next), (2, row_prev)):
            @pl.when(needs_b(s, row, c, a, b))
            def _(s=s, row=row):
                b_copy(s, a, b, row, b_in.at[0, b]).wait_send()

        @pl.when((core == 1) & needs_b(3, row_prev2, c, a, b))
        def _():
            b_copy(3, a, b, row_prev2, b_in.at[0, b]).wait_send()

        @pl.when((core == 1) & needs_b(2, r, c, a, b))
        def _():
            hand_b(a, b).wait_send()
        pltpu.make_async_copy(w.at[a, b], out.at[a, b], out_sem.at[a, b]).wait()
    each_ab(drain_b)

    def drain_x(s, carry):
        for q in range(PIECES):
            collect(col_route(s, q)[1])
            for a in range(2):
                collect(row_route(s, a, q)[1])
        return carry
    lax.fori_loop(0, FRONTS, drain_x, 0)


def shards(n_row, n_col, upper_a, upper_b, right_side, a_bases, b_bases, a_values, b_values):
    nb = upper_a.shape[1]
    bf16, f32 = jnp.bfloat16, jnp.float32
    b_tiles = jnp.transpose(upper_b, (0, 2, 1, 3))
    c_tiles = jnp.transpose(right_side, (0, 2, 1, 3))
    dma = pltpu.SemaphoreType.DMA
    solved = pl.pallas_call(
        functools.partial(plan, nb, n_row, n_col),
        out_shape=jax.ShapeDtypeStruct((2, 2, nb, nb), f32),
        in_specs=[pl.BlockSpec(memory_space=pl.ANY)] * 7,
        out_specs=pl.BlockSpec(memory_space=pl.ANY),
        scratch_shapes=[
            pltpu.VMEM((FRONTS, 2, nb, nb), bf16),
            pltpu.VMEM((FRONTS, 2, 2, nb, nb), bf16),
            pltpu.VMEM((FRONTS, nb, nb), bf16),
            pltpu.VMEM((FRONTS, 2, nb, nb), bf16),
            pltpu.VMEM((2, 2, nb, nb), f32),
            pltpu.VMEM((2, 2, nb, nb), bf16),
            pltpu.VMEM((nb, nb), bf16),
            pltpu.VMEM((nb, nb), bf16),
            pltpu.VMEM((nb, nb), bf16),
            pltpu.VMEM((nb, nb), f32),
            pltpu.VMEM((2, nb, nb), bf16),
            pltpu.VMEM((1, nb), f32),
            pltpu.VMEM((1, nb), f32),
            dma((5,)),
            dma((2, 2)),
            dma((FRONTS, 2)),
            dma((FRONTS, 2, 2)),
            dma((FRONTS, 2)),
            dma((FRONTS, 2, 2)),
            dma((FRONTS, PIECES, 3)),
            dma((FRONTS, 2, PIECES, 5)),
            dma((FRONTS, PIECES)),
            dma((FRONTS, 2, PIECES)),
        ],
        compiler_params=pltpu.CompilerParams(
            collective_id=0, has_side_effects=True, vmem_limit_bytes=60 * 1024 * 1024
        ),
    )(upper_a, b_tiles, c_tiles, a_bases, b_bases, a_values[:, None, :], b_values[:, None, :])
    return jnp.transpose(solved, (0, 2, 1, 3))


def solution(mesh):
    return jax.shard_map(
        functools.partial(shards, mesh.shape["row"], mesh.shape["col"]),
        mesh=mesh,
        in_specs=(
            P(None, "row", "col"),
            P(None, "row", None, "col"),
            P(None, "row", None, "col"),
            P(None, "row", None),
            P(None, "col", None),
            P(None, "row"),
            P(None, "col"),
        ),
        out_specs=P(None, "row", None, "col"),
        check_vma=False,
    )
```

time: 494 us -> 165 us (0.33)
  the two profiles are of different devices: /device:TPU:76 before, /device:TPU:0 now
where the time goes in v1:
time: 165 us
  Pallas kernels  148 us (90%)
  local copies, waits for them, and re-layouts  16.2 us (10%)
    pallas_call x1, Pallas kernels, shards(): pl.pallas_call(functools.partial(plan, nb, n_row, n_col), out_shape=jax.S...  148 us
    transpose x1, local copies, waits for them, and re-layouts, shards(): return jnp.transpose(solved, (0, 2, 1, 3))  7.44 us
    unnamed x4, local copies, waits for them, and re-layouts  6.03 us

profile of v1, /device:TPU:0, one launch (start us, length us, event | category | flops | bytes accessed | tf_op | source)
XLA Modules:
  0.0 164.6 jit_solution(5047306954979633105)
XLA Ops:
  0.0 0.0 copy-start
  0.0 1.4 broadcast_in_dim.6.av_in
  1.4 1.3 broadcast_in_dim.7.bv_in
  2.7 3.3 %copy.14 = bf16[2,512,2,512]{3,1,2,0:T(8,128)(2,1)} copy(bf16[2,512,2,512]{3,2,1,0:T(2,128)(2,1)} %param.9) | data formatting | bytes 4194304 | tf_op args[2]
  6.0 0.0 copy-done
  6.0 2.8 %copy.13 = bf16[4,512,2,512]{3,1,2,0:T(8,128)(2,1)} copy(bf16[4,512,2,512]{3,2,1,0:T(2,128)(2,1)S(1)} %copy-done) | data formatting | bytes 8388608 | tf_op args[1]
  8.7 148.4 %shard_map.73 = f32[2,2,512,512]{3,2,1,0:T(8,128)} custom-call(bf16[2,512,512]{2,1,0:T(8,128)(2,1)} %a_in.1, bf16[4,2,512,512]{3,2,1,0:T(8,128)(2,1)} %bitcast.8, bf16[2,2,512,512]{3,2,1,0:T(8,128)(2,1)} %bitcast.9, bf16[2,512,512]{2,1,0:T(8,128)(2,1)} %qa_in.1, bf16[2,512,512]{2,1,0:T(8,128)(2,1)} %qb_in.1, f32[2,1,512]{2,1,0:T(1,128)} %broadcast_in_dim.6.av_in, ...), custom_call_target="tpu_custom_call" | custom-call | tf_op jit(solution)/shard_map/pallas_call | solution.py:380
  157.1 7.4 %copy.10 = f32[2,512,2,512]{3,2,1,0:T(2,128)} copy(f32[2,512,2,512]{3,1,2,0:T(8,128)} %bitcast.7) | data formatting | bytes 8388608 | tf_op jit(solution)/shard_map/transpose | solution.py:414
Async XLA Ops:
  0.0 6.0 %copy-start = (bf16[4,512,2,512]{3,2,1,0:T(2,128)(2,1)S(1)}, bf16[4,512,2,512]{3,2,1,0:T(2,128)(2,1)}, u32[]{:S(2)}) copy-start(bf16[4,512,2,512]{3,2,1,0:T(2,128)(2,1)} %param.8) | copy-start | bytes 12582916

commit v2 on v1

--- a/solution.py
+++ b/solution.py
@@ -10,7 +10,7 @@
 MESH = pl.DeviceIdType.MESH
 FRONTS = 4
 RING = 4
-PIECES = 2
+PIECES = 4
 
 
 def plan(nb, n_row, n_col, a_in, b_in, c_in, qa_in, qb_in, av_in, bv_in, out,
@@ -31,6 +31,8 @@
 
     col_next = mod(c + 1, n_col)
     col_prev = mod(c + n_col - 1, n_col)
+    col_next2 = mod(c + 2, n_col)
+    col_prev2 = mod(c + n_col - 2, n_col)
 
     shift = mod(c - r + 1 + n_col, n_col)
     turn = mod(shift, 8)
@@ -76,12 +78,11 @@
             for b in range(2):
                 fn(a, b)
 
-    def send_a(s, col):
-        def one(a):
+    def send_a(s, col, tiles=(0, 1)):
+        for a in tiles:
             @pl.when(needs_a(s, r, col, a))
-            def _():
+            def _(a=a):
                 a_copy(s, a, col, a_in.at[a]).start()
-        each_a(one)
 
     def send_b(s, row):
         def one(a, b):
@@ -96,8 +97,11 @@
     row_prev2 = mod(r + n_row - 2, n_row)
     partner = y * 2 + 1 - core
 
+    def piece_of(q):
+        return pl.ds(pl.multiple_of(q * rows, rows), rows), 1 - 2 * mod(q, 2)
+
     def col_route(s, q):
-        g = 1 if q % 2 == 0 else -1
+        piece, g = piece_of(q)
         k = k_of(s, c)
         rr = mod(k, 8)
         ry = rr // 2
@@ -105,7 +109,6 @@
         root = valid & (r == rr)
         oy = mod((y - ry) * g + RING, RING)
         relay = valid & (oy != 0) & (core == 1)
-        piece = pl.ds(q * rows, rows)
 
         def copy(n, row):
             return remote(xc.at[s, piece], xc.at[s, piece], xc_send.at[s, q, n], xc_recv.at[s, q], row, c)
@@ -115,10 +118,10 @@
             (root, copy(1, row_of(y - g, 1))),
             (root | relay, copy(2, partner)),
         ]
-        return valid & (r != rr), sends, copy(2, partner)
+        return valid & (r != rr), sends
 
     def row_route(s, a, q):
-        g = 1 if q % 2 == 0 else -1
+        piece, g = piece_of(q)
         l = r + 8 * a - 1 + s
         valid = l >= 0
         lc = mod(l + n_col, n_col)
@@ -126,26 +129,27 @@
         root = valid & (c == lc)
         oz = mod((z - rz) * g + RING, RING)
         ox = mod((x - rx) * g + RING, RING)
-        early = (rz == RING - 1) & (z == 0) & (ox == 0)
-        forth = valid & ((ox == 0) | (ox == 1))
-        back = valid & (ox == 0)
-        if g == 1:
-            forth = forth & jnp.logical_not(early)
-        else:
-            back = back & jnp.logical_not(early)
-        piece = pl.ds(q * rows, rows)
+        jump = rz == RING - 1
+        jump_to = mod(lc + 1, n_col)
 
         def copy(n, col):
             return remote(xr.at[s, a, piece], xr.at[s, a, piece], xr_send.at[s, a, q, n], xr_recv.at[s, a, q], r, col)
 
+        def step(when, n, col):
+            return valid & when & jnp.logical_not(jump & (col == jump_to)), copy(n, col)
+
+        turned = core > 1
+        one, two = jnp.where(turned, ox, oz), jnp.where(turned, oz, ox)
+        z_forth, z_back = col_of(x, z + g), col_of(x, z - g)
+        x_forth, x_back = col_of(x + g, z), col_of(x - g, z)
         sends = [
-            (valid & (ox == 0) & ((oz == 0) | (oz == 1)), copy(0, col_of(x, z + g))),
-            (root & (rz == RING - 1), copy(4, col_next)),
-            (valid & (ox == 0) & (oz == 0), copy(1, col_of(x, z - g))),
-            (forth, copy(2, col_of(x + g, z))),
-            (back, copy(3, col_of(x - g, z))),
+            (root & jump, copy(4, col_next)),
+            step((two == 0) & ((one == 0) | (one == 1)), 0, jnp.where(turned, x_forth, z_forth)),
+            step((two == 0) & (one == 0), 1, jnp.where(turned, x_back, z_back)),
+            step((two == 0) | (two == 1), 2, jnp.where(turned, z_forth, x_forth)),
+            step(two == 0, 3, jnp.where(turned, z_back, x_back)),
         ]
-        return valid & (c != lc), sends, copy(0, col_of(x, z + g))
+        return valid & (c != lc), sends
 
     def launch(sends):
         for when, copy in sends:
@@ -159,66 +163,72 @@
             def _(copy=copy):
                 copy.wait_send()
 
-    def take_col(s):
-        for q in range(PIECES):
-            arrives, sends, copy = col_route(s, q)
-
-            @pl.when(arrives)
-            def _():
-                copy.wait_recv()
-                launch(sends)
-
-    def take_row(s, a):
-        for q in range(PIECES):
-            arrives, sends, copy = row_route(s, a, q)
-
-            @pl.when(arrives)
-            def _():
-                copy.wait_recv()
-                launch(sends)
+    def take(route):
+        arrives, sends = route
+
+        @pl.when(arrives)
+        def _():
+            sends[-1][1].wait_recv()
+            launch(sends)
+
+    def each_piece(fn):
+        def body(q, carry):
+            fn(q)
+            return carry
+        lax.fori_loop(0, PIECES, body, 0)
 
     f32 = jnp.float32
 
     def matmul(p, q):
         return jnp.dot(p, q, preferred_element_type=f32)
 
-    def update(s, a, b):
+    def update_col(s, a, b):
         i, j = r + 8 * a, c + n_col * b
         k = j + 1 - s
 
         @pl.when((k >= 0) & (k < n_col) & (i < k))
         def _():
-            @pl.when(s != 2)
-            def _():
-                a_copy(s, a, c, a_buf.at[s, a]).wait_recv()
+            a_copy(s, a, c, a_buf.at[s, a]).wait_recv()
             w[a, b] = w[a, b] - matmul(a_buf[s, a], xc[s])
 
+    def update_row(s, a, b):
         @pl.when(needs_b(s, r, c, a, b))
         def _():
             @pl.when(s != 2)
             def _():
                 b_copy(s, a, b, r, b_buf.at[s, a, b]).wait_recv()
             w[a, b] = w[a, b] - matmul(xr[s, a], b_buf[s, a, b])
+
+    def hand_on():
+        def one(a, b):
+            @pl.when(needs_b(2, r, c, a, b))
+            def _():
+                b_copy(2, a, b, r, b_buf.at[2, a, b]).wait_recv()
+
+                @pl.when(core == 1)
+                def _():
+                    hand_b(a, b).start()
+        each_ab(one)
 
     def solve(s):
         half[0] = w[a_own, b_own].astype(jnp.bfloat16)
         half[1] = matmul(qat[...], half[0]).astype(jnp.bfloat16)
         half[0] = (matmul(half[1], qb[...]) * inv[...]).astype(jnp.bfloat16)
-        for q in range(PIECES):
-            piece = pl.ds(q * rows, rows)
+
+        def finish(q):
+            piece, _ = piece_of(q)
             left = matmul(qa[piece, :], half[0]).astype(jnp.bfloat16)
             tile = lax.dot_general(left, qb[...], (((1,), (1,)), ((), ())), preferred_element_type=f32)
             tile = tile.astype(jnp.bfloat16)
             xr[s, a_own, piece, :] = tile
             xc[s, piece, :] = tile
             w[a_own, b_own, piece, :] = tile.astype(f32)
-            _, sends, _ = col_route(s, q)
-            launch(sends)
-            _, sends, _ = row_route(s, a_own, q)
-            launch(sends)
+            launch(row_route(s, a_own, q)[1])
+            launch(col_route(s, q)[1])
+        each_piece(finish)
 
     barrier = pltpu.get_barrier_semaphore()
-    friends = [(partner, c), (r, col_next), (r, col_prev)]
+    friends = [(partner, c), (r, col_next), (r, col_prev), (r, col_next2), (r, col_prev2)]
     for d in (1, -1):
         friends += [(row_of(y + d, 0), c), (row_of(y + d, 1), c), (r, col_of(x, z + d)), (r, col_of(x + d, z))]
     for friend in friends:
@@ -228,8 +238,8 @@
         pltpu.make_async_copy(c_in, c_buf, local_sem.at[0]),
         pltpu.make_async_copy(qa_in.at[a_own], qa, local_sem.at[1]),
         pltpu.make_async_copy(qb_in.at[b_own], qb, local_sem.at[2]),
-        pltpu.make_async_copy(av_in.at[a_own], av, local_sem.at[3]),
-        pltpu.make_async_copy(bv_in.at[b_own], bv, local_sem.at[4]),
+        pltpu.make_async_copy(av_in, av, local_sem.at[3]),
+        pltpu.make_async_copy(bv_in, bv, local_sem.at[4]),
     ]
     for load in loads:
         load.start()
@@ -244,103 +254,135 @@
     each_ab(lambda a, b: pl.when(needs_b(1, r, c, a, b))(lambda: local_b(a, b).start()))
 
     pl.semaphore_wait(barrier, len(friends))
-    send_a(0, col_prev)
-    send_b(0, row_next)
-
     for load in loads:
         load.wait()
 
     @pl.when(solves)
     def _():
         qat[...] = qa[...].T
-        down = jnp.broadcast_to(av[...], (128, nb)).T
+        down = jnp.broadcast_to(jnp.where(a_own == 0, av[0:1, :], av[1:2, :]), (128, nb)).T
+        across = jnp.where(b_own == 0, bv[0:1, :], bv[1:2, :])
         for n in range(nb // 128):
             lanes = pl.ds(n * 128, 128)
-            inv[:, lanes] = 1.0 / (down + bv[:, lanes])
+            inv[:, lanes] = 1.0 / (down + across[:, n * 128:n * 128 + 128])
 
     def load_w(t, carry):
         w[t // 2, t % 2] = c_buf[t // 2, t % 2].astype(f32)
         return carry
     lax.fori_loop(0, 4, load_w, 0)
 
+    def near(s):
+        l = mod(r - 1 + s + n_col, n_col)
+        gap = mod(x - l // RING + RING, RING)
+        return jnp.where((gap == 0) | (gap == 1), 0, 1), ((gap == 0) | (gap == 2))
+
+    def far(p):
+        a_first, _ = near(p)
+        each_piece(lambda q: take(row_route(p, 1 - a_first, q)))
+
+    def settled(p, a, b):
+        return solves & (turn > p) & (a == a_own) & (b == b_own)
+
+    def put_off(p, a):
+        a_first, centre = near(p)
+        return centre & (a != a_first)
+
+    def stream(t):
+        h = mod(shift, 8)
+
+        def when(point, send):
+            pl.when(t == point)(send)
+
+        when(jnp.where(h == 7, 1, 0), lambda: send_a(0, col_prev))
+        when(jnp.where((core == 1) & ((h == 5) | (h == 6)), 1, 0), lambda: send_b(0, row_next))
+        when(jnp.where(h == 1, 1, 0), lambda: send_a(2, col_next))
+        when(jnp.where((core == 0) & (h == 1), 1, 0), lambda: send_b(2, row_prev))
+        late = (core == 0) & (z > 1)
+        when(jnp.where(late, 2, jnp.where(h == 1, 1, jnp.where(h == 2, 2, 0))), lambda: send_a(3, col_next2, (0,)))
+        when(jnp.where(late, 3, jnp.where(h == 1, 1, jnp.where(h == 2, 2, 0))), lambda: send_a(3, col_next2, (1,)))
+
+        @pl.when(core == 1)
+        def _():
+            when(jnp.where(h == 0, 2, jnp.where(h == 1, 3, 0)), lambda: send_b(3, row_prev2))
+
     def front(t, carry):
         s = t - 1
 
         @pl.when(t > 0)
         def _():
-            take_col(s)
-            take_row(s, jnp.where(solves, a_own, a_near(s)))
-
-        ahead = turn == t
-
-        @pl.when(ahead)
-        def _():
-            @pl.when(t > 0)
-            def _():
-                update(s, a_own, b_own)
+            a, centre = near(s)
+            ahead = solves & (turn >= t)
+
+            @pl.when(centre | ahead)
+            def _():
+                def both(q):
+                    take(row_route(s, a, q))
+                    take(col_route(s, q))
+                each_piece(both)
+
+            @pl.when(jnp.logical_not(centre | ahead))
+            def _():
+                each_piece(lambda q: take(col_route(s, q)))
+
+                def both(q):
+                    take(row_route(s, a, q))
+                    take(row_route(s, 1 - a, q))
+                each_piece(both)
+
+            pl.when((t == 3) & (turn == 3))(hand_on)
+
+            @pl.when(ahead)
+            def _():
+                update_col(s, a_own, b_own)
+                update_row(s, a_own, b_own)
+
+        @pl.when(turn == t)
+        def _():
             solve(t)
 
-        @pl.when(t == 1)
-        def _():
-            send_a(2, col_next)
-            send_b(2, row_prev)
-
-        @pl.when(t > 0)
-        def _():
-            take_row(s, 1 - jnp.where(solves, a_own, a_near(s)))
-
-            def rest(n, carry):
-                a, b = n // 2, n % 2
-
-                @pl.when(jnp.logical_not(ahead & (a == a_own) & (b == b_own)))
+            def catch_up(p, carry):
+                pl.when(jnp.logical_not(near(p)[1]))(lambda: far(p))
+                return carry
+            lax.fori_loop(0, t, catch_up, 0)
+
+        stream(t)
+        pl.when((t == 3) & (turn != 3))(hand_on)
+
+        def rest(m, carry):
+            p = jnp.where(t == FRONTS, jnp.where(m < 2, 2 * m, FRONTS - 1), 1)
+
+            def one(n, carry):
+                a, b = n // 2, mod(n, 2)
+
+                @pl.when(jnp.logical_not(settled(p, a, b)))
                 def _():
-                    update(s, a, b)
-
-                @pl.when(t == FRONTS)
-                def _():
-                    pltpu.make_async_copy(w.at[a, b], out.at[a, b], out_sem.at[a, b]).start()
+                    update_col(p, a, b)
+                    pl.when(jnp.logical_not(put_off(p, a)))(lambda: update_row(p, a, b))
                 return carry
-            lax.fori_loop(0, 4, rest, 0)
-
-        @pl.when(t == 2)
-        def _():
-            relay_two()
+            return lax.fori_loop(0, 4, one, carry)
+        lax.fori_loop(0, jnp.where(t == FRONTS, 3, jnp.where(t == 3, 1, 0)), rest, 0)
         return carry
 
-    def a_near(s):
-        l = mod(r - 1 + s + n_col, n_col)
-        gap = mod(x - l // RING + RING, RING)
-        return jnp.where((gap == 0) | (gap == 1), 0, 1)
-
-    def relay_two():
-        def one(a):
-            @pl.when(needs_a(2, r, c, a))
-            def _():
-                a_copy(2, a, c, a_buf.at[2, a]).wait_recv()
-
-            @pl.when(needs_a(3, r, col_next, a))
-            def _():
-                a_copy(3, a, col_next, a_buf.at[2, a]).start()
-        each_a(one)
-
-        @pl.when(core == 1)
-        def _():
-            send_b(3, row_prev2)
-
-        def pair(a, b):
-            @pl.when(needs_b(2, r, c, a, b))
-            def _():
-                b_copy(2, a, b, r, b_buf.at[2, a, b]).wait_recv()
-
-                @pl.when(core == 1)
-                def _():
-                    hand_b(a, b).start()
-        each_ab(pair)
-
     lax.fori_loop(0, FRONTS + 1, front, 0)
 
+    def last(n, carry):
+        a_first, _ = near(FRONTS - 1)
+        a = jnp.where(n < 2, a_first, 1 - a_first)
+        b = mod(n, 2)
+
+        def one(p, carry):
+            @pl.when(put_off(p, a))
+            def _():
+                pl.when(b == 0)(lambda: far(p))
+                pl.when(jnp.logical_not(settled(p, a, b)))(lambda: update_row(p, a, b))
+            return carry
+        lax.fori_loop(0, FRONTS, one, 0)
+        pltpu.make_async_copy(w.at[a, b], out.at[a, b], out_sem.at[a, b]).start()
+        return carry
+    lax.fori_loop(0, 4, last, 0)
+
     def drain_a(a):
-        for s, col in ((0, col_prev), (2, col_next), (3, col_next)):
+        for s, col in ((0, col_prev), (2, col_next), (3, col_next2)):
             @pl.when(needs_a(s, r, col, a))
             def _(s=s, col=col):
                 a_copy(s, a, col, a_in.at[a]).wait_send()
@@ -363,10 +405,11 @@
     each_ab(drain_b)
 
     def drain_x(s, carry):
-        for q in range(PIECES):
+        def one(q):
             collect(col_route(s, q)[1])
             for a in range(2):
                 collect(row_route(s, a, q)[1])
+        each_piece(one)
         return carry
     lax.fori_loop(0, FRONTS, drain_x, 0)
 
@@ -394,8 +437,8 @@
             pltpu.VMEM((nb, nb), bf16),
             pltpu.VMEM((nb, nb), f32),
             pltpu.VMEM((2, nb, nb), bf16),
-            pltpu.VMEM((1, nb), f32),
-            pltpu.VMEM((1, nb), f32),
+            pltpu.VMEM((2, nb), f32),
+            pltpu.VMEM((2, nb), f32),
             dma((5,)),
             dma((2, 2)),
             dma((FRONTS, 2)),
@@ -410,7 +453,7 @@
         compiler_params=pltpu.CompilerParams(
             collective_id=0, has_side_effects=True, vmem_limit_bytes=60 * 1024 * 1024
         ),
-    )(upper_a, b_tiles, c_tiles, a_bases, b_bases, a_values[:, None, :], b_values[:, None, :])
+    )(upper_a, b_tiles, c_tiles, a_bases, b_bases, a_values, b_values)
     return jnp.transpose(solved, (0, 2, 1, 3))
 
 

time: 165 us -> 135 us (0.82)
  the two profiles are of different devices: /device:TPU:0 before, /device:TPU:76 now
where the time goes in v2:
time: 135 us
  Pallas kernels  122 us (90%)
  local copies, waits for them, and re-layouts  13.6 us (10%)
    pallas_call x1, Pallas kernels, shards(): pl.pallas_call(functools.partial(plan, nb, n_row, n_col), out_shape=jax.S...  122 us
    transpose x1, local copies, waits for them, and re-layouts, shards(): return jnp.transpose(solved, (0, 2, 1, 3))  7.44 us
    unnamed x4, local copies, waits for them, and re-layouts  6.18 us

profile of v2, /device:TPU:76, one launch (start us, length us, event | category | flops | bytes accessed | tf_op | source)
XLA Modules:
  0.0 135.3 jit_solution(5196498380388336821)
XLA Ops:
  0.0 0.0 copy-start
  0.0 3.4 %copy.14 = bf16[2,512,2,512]{3,1,2,0:T(8,128)(2,1)} copy(bf16[2,512,2,512]{3,2,1,0:T(2,128)(2,1)} %param.9) | data formatting | bytes 4194304 | tf_op args[2]
  3.4 0.0 copy-done
  3.4 2.8 %copy.13 = bf16[4,512,2,512]{3,1,2,0:T(8,128)(2,1)} copy(bf16[4,512,2,512]{3,2,1,0:T(2,128)(2,1)S(1)} %copy-done) | data formatting | bytes 8388608 | tf_op args[1]
  6.2 121.7 %shard_map.73 = f32[2,2,512,512]{3,2,1,0:T(8,128)} custom-call(bf16[2,512,512]{2,1,0:T(8,128)(2,1)} %a_in.1, bf16[4,2,512,512]{3,2,1,0:T(8,128)(2,1)} %bitcast.8, bf16[2,2,512,512]{3,2,1,0:T(8,128)(2,1)} %bitcast.9, bf16[2,512,512]{2,1,0:T(8,128)(2,1)} %qa_in.1, bf16[2,512,512]{2,1,0:T(8,128)(2,1)} %qb_in.1, f32[2,512]{1,0:T(2,128)} %av_in.1, f32[2,512]{1,0:T(2,128)} %bv_in.1), custom_call_target="tpu_custom_call" | custom-call | tf_op jit(solution)/shard_map/pallas_call | solution.py:423
  127.9 7.4 %copy.10 = f32[2,512,2,512]{3,2,1,0:T(2,128)} copy(f32[2,512,2,512]{3,1,2,0:T(8,128)} %bitcast.7) | data formatting | bytes 8388608 | tf_op jit(solution)/shard_map/transpose | solution.py:457
Async XLA Ops:
  0.0 3.4 %copy-start = (bf16[4,512,2,512]{3,2,1,0:T(2,128)(2,1)S(1)}, bf16[4,512,2,512]{3,2,1,0:T(2,128)(2,1)}, u32[]{:S(2)}) copy-start(bf16[4,512,2,512]{3,2,1,0:T(2,128)(2,1)} %param.8) | copy-start | bytes 12582916

commit v3 on v2

--- a/solution.py
+++ b/solution.py
@@ -10,7 +10,7 @@
 MESH = pl.DeviceIdType.MESH
 FRONTS = 4
 RING = 4
-PIECES = 4
+PIECES = 2
 
 
 def plan(nb, n_row, n_col, a_in, b_in, c_in, qa_in, qb_in, av_in, bv_in, out,
@@ -41,6 +41,7 @@
     b_own = jnp.where(l_own >= n_col, 1, 0)
     solves = (turn < FRONTS) & (l_own >= 0)
     turn = jnp.where(solves, turn, 99)
+    leaps = solves & (z == RING - 1)
 
     def remote(src, dst, send, recv, row, col):
         return pltpu.make_async_remote_copy(
@@ -101,22 +102,22 @@
         return pl.ds(pl.multiple_of(q * rows, rows), rows), 1 - 2 * mod(q, 2)
 
     def col_route(s, q):
-        piece, g = piece_of(q)
+        piece, _ = piece_of(q)
         k = k_of(s, c)
         rr = mod(k, 8)
         ry = rr // 2
         valid = has_col(s, c)
         root = valid & (r == rr)
-        oy = mod((y - ry) * g + RING, RING)
-        relay = valid & (oy != 0) & (core == 1)
+        oy = mod(y - ry + RING, RING)
+        lands = valid & jnp.where(oy == RING - 1, core == 1, (oy != 0) & (core == 0))
 
         def copy(n, row):
             return remote(xc.at[s, piece], xc.at[s, piece], xc_send.at[s, q, n], xc_recv.at[s, q], row, c)
 
         sends = [
-            (root | (relay & (oy == 1)), copy(0, row_of(y + g, 1))),
-            (root, copy(1, row_of(y - g, 1))),
-            (root | relay, copy(2, partner)),
+            (root, copy(1, row_of(y - 1, 1))),
+            (root | lands, copy(2, partner)),
+            (root | (lands & (oy == 1)), copy(0, row_of(y + 1, 0))),
         ]
         return valid & (r != rr), sends
 
@@ -135,25 +136,25 @@
         def copy(n, col):
             return remote(xr.at[s, a, piece], xr.at[s, a, piece], xr_send.at[s, a, q, n], xr_recv.at[s, a, q], r, col)
 
-        def step(when, n, col):
-            return valid & when & jnp.logical_not(jump & (col == jump_to)), copy(n, col)
-
-        turned = core > 1
-        one, two = jnp.where(turned, ox, oz), jnp.where(turned, oz, ox)
-        z_forth, z_back = col_of(x, z + g), col_of(x, z - g)
-        x_forth, x_back = col_of(x + g, z), col_of(x - g, z)
+        def step(offset, ahead, when, n, col):
+            go = when & ((offset == 0) | (ahead & (offset == 1)))
+            return valid & go & jnp.logical_not(jump & (col == jump_to)), copy(n, col)
+
         sends = [
             (root & jump, copy(4, col_next)),
-            step((two == 0) & ((one == 0) | (one == 1)), 0, jnp.where(turned, x_forth, z_forth)),
-            step((two == 0) & (one == 0), 1, jnp.where(turned, x_back, z_back)),
-            step((two == 0) | (two == 1), 2, jnp.where(turned, z_forth, x_forth)),
-            step(two == 0, 3, jnp.where(turned, z_back, x_back)),
+            step(oz, g == 1, ox == 0, 0, col_of(x, z + 1)),
+            step(oz, g == -1, ox == 0, 1, col_of(x, z - 1)),
+            step(ox, g == 1, valid, 2, col_of(x + 1, z)),
+            step(ox, g == -1, valid, 3, col_of(x - 1, z)),
         ]
         return valid & (c != lc), sends
 
-    def launch(sends):
-        for when, copy in sends:
-            @pl.when(when)
+    def launch(sends, held=False, only=(0, 1, 2, 3, 4), hold=()):
+        for n, (when, copy) in enumerate(sends):
+            if n not in only:
+                continue
+
+            @pl.when(when & jnp.logical_not(held) if n in hold else when)
             def _(copy=copy):
                 copy.start()
 
@@ -223,9 +224,13 @@
             xr[s, a_own, piece, :] = tile
             xc[s, piece, :] = tile
             w[a_own, b_own, piece, :] = tile.astype(f32)
-            launch(row_route(s, a_own, q)[1])
+            launch(row_route(s, a_own, q)[1], leaps, hold=(1, 3))
             launch(col_route(s, q)[1])
         each_piece(finish)
+
+        @pl.when(leaps)
+        def _():
+            each_piece(lambda q: launch(row_route(s, a_own, q)[1], only=(1, 3)))
 
     barrier = pltpu.get_barrier_semaphore()
     friends = [(partner, c), (r, col_next), (r, col_prev), (r, col_next2), (r, col_prev2)]
@@ -294,7 +299,7 @@
             pl.when(t == point)(send)
 
         when(jnp.where(h == 7, 1, 0), lambda: send_a(0, col_prev))
-        when(jnp.where((core == 1) & ((h == 5) | (h == 6)), 1, 0), lambda: send_b(0, row_next))
+        when(0, lambda: send_b(0, row_next))
         when(jnp.where(h == 1, 1, 0), lambda: send_a(2, col_next))
         when(jnp.where((core == 0) & (h == 1), 1, 0), lambda: send_b(2, row_prev))
         late = (core == 0) & (z > 1)
@@ -377,7 +382,7 @@
                 pl.when(jnp.logical_not(settled(p, a, b)))(lambda: update_row(p, a, b))
             return carry
         lax.fori_loop(0, FRONTS, one, 0)
-        pltpu.make_async_copy(w.at[a, b], out.at[a, b], out_sem.at[a, b]).start()
+        pltpu.make_async_copy(w.at[a, b], out.at[a, :, b], out_sem.at[a, b]).start()
         return carry
     lax.fori_loop(0, 4, last, 0)
 
@@ -401,7 +406,7 @@
         @pl.when((core == 1) & needs_b(2, r, c, a, b))
         def _():
             hand_b(a, b).wait_send()
-        pltpu.make_async_copy(w.at[a, b], out.at[a, b], out_sem.at[a, b]).wait()
+        pltpu.make_async_copy(w.at[a, b], out.at[a, :, b], out_sem.at[a, b]).wait()
     each_ab(drain_b)
 
     def drain_x(s, carry):
@@ -417,12 +422,12 @@
 def shards(n_row, n_col, upper_a, upper_b, right_side, a_bases, b_bases, a_values, b_values):
     nb = upper_a.shape[1]
     bf16, f32 = jnp.bfloat16, jnp.float32
-    b_tiles = jnp.transpose(upper_b, (0, 2, 1, 3))
+    b_tiles = jnp.transpose(upper_b[:3], (0, 2, 1, 3))
     c_tiles = jnp.transpose(right_side, (0, 2, 1, 3))
     dma = pltpu.SemaphoreType.DMA
     solved = pl.pallas_call(
         functools.partial(plan, nb, n_row, n_col),
-        out_shape=jax.ShapeDtypeStruct((2, 2, nb, nb), f32),
+        out_shape=jax.ShapeDtypeStruct((2, nb, 2, nb), f32),
         in_specs=[pl.BlockSpec(memory_space=pl.ANY)] * 7,
         out_specs=pl.BlockSpec(memory_space=pl.ANY),
         scratch_shapes=[
@@ -454,7 +459,7 @@
             collective_id=0, has_side_effects=True, vmem_limit_bytes=60 * 1024 * 1024
         ),
     )(upper_a, b_tiles, c_tiles, a_bases, b_bases, a_values, b_values)
-    return jnp.transpose(solved, (0, 2, 1, 3))
+    return solved
 
 
 def solution(mesh):

time: 135 us -> 131 us (0.970)
  Pallas kernels: 122 us -> 118 us
    transpose x1 -> x0, local copies, waits for them, and re-layouts: 7.44 us -> none  [shards(): return jnp.transpose(solved, (0, 2, 1, 3))]
    unnamed x4 -> x3, local copies, waits for them, and re-layouts: 6.18 us -> 11.1 us
    pallas_call x1, Pallas kernels: 122 us -> 118 us  [shards(): pl.pallas_call(functools.partial(plan, nb, n_row, n_col), out_shape=jax.S...]
    slice x0 -> x2, local copies, waits for them, and re-layouts: none -> 1.89 us  [shards(): b_tiles = jnp.transpose(upper_b[:3], (0, 2, 1, 3))]
where the time goes in v3:
time: 131 us
  Pallas kernels  118 us (90%)
  local copies, waits for them, and re-layouts  13 us (10%)
    pallas_call x1, Pallas kernels, shards(): pl.pallas_call(functools.partial(plan, nb, n_row, n_col), out_shape=jax.S...  118 us
    unnamed x3, local copies, waits for them, and re-layouts  11.1 us

profile of v3, /device:TPU:76, one launch (start us, length us, event | category | flops | bytes accessed | tf_op | source)
XLA Modules:
  0.0 130.9 jit_solution(18055057610269747765)
XLA Ops:
  0.0 3.3 %copy.14 = bf16[2,512,2,512]{3,1,2,0:T(8,128)(2,1)} copy(bf16[2,512,2,512]{3,2,1,0:T(2,128)(2,1)} %param.9) | data formatting | bytes 4194304 | tf_op args[2]
  3.3 0.0 slice-start
  3.3 1.9 %slice-done = bf16[3,512,2,512]{3,2,1,0:T(2,128)(2,1)S(1)} async-done(((bf16[4,512,2,512]{3,2,1,0:T(2,128)(2,1)}), bf16[3,512,2,512]{3,2,1,0:T(2,128)(2,1)S(1)}, s32[]{:S(2)}) %slice-start) | async-done | bytes 3145752 | tf_op jit(solution)/shard_map/slice | solution.py:425
  5.1 2.2 %copy.13 = bf16[3,512,2,512]{3,1,2,0:T(8,128)(2,1)} copy(bf16[3,512,2,512]{3,2,1,0:T(2,128)(2,1)S(1)} %slice-done) | data formatting | bytes 6291456
  7.4 117.9 %shard_map.73 = f32[2,512,2,512]{3,2,1,0:T(2,128)} custom-call(bf16[2,512,512]{2,1,0:T(8,128)(2,1)} %a_in.1, bf16[3,2,512,512]{3,2,1,0:T(8,128)(2,1)} %bitcast.6, bf16[2,2,512,512]{3,2,1,0:T(8,128)(2,1)} %bitcast.7, bf16[2,512,512]{2,1,0:T(8,128)(2,1)} %qa_in.1, bf16[2,512,512]{2,1,0:T(8,128)(2,1)} %qb_in.1, f32[2,512]{1,0:T(2,128)} %av_in.1, f32[2,512]{1,0:T(2,128)} %bv_in.1), custom_call_target="tpu_custom_call" | custom-call | tf_op jit(solution)/shard_map/pallas_call | solution.py:428
  125.3 5.6 %copy.16 = f32[2,512,2,512]{3,2,1,0:T(2,128)} copy(f32[2,512,2,512]{3,2,1,0:T(2,128)} %shard_map.73) | data formatting | bytes 8388608
Async XLA Ops:
  3.3 1.9 %slice-start = ((bf16[4,512,2,512]{3,2,1,0:T(2,128)(2,1)}), bf16[3,512,2,512]{3,2,1,0:T(2,128)(2,1)S(1)}, s32[]{:S(2)}) async-start(bf16[4,512,2,512]{3,2,1,0:T(2,128)(2,1)} %param.8), calls=%async_computation | async-start | bytes 6291456 | tf_op jit(solution)/shard_map/slice | solution.py:425

commit v4 on v3

--- a/solution.py
+++ b/solution.py
@@ -189,7 +189,9 @@
 
         @pl.when((k >= 0) & (k < n_col) & (i < k))
         def _():
-            a_copy(s, a, c, a_buf.at[s, a]).wait_recv()
+            @pl.when(s != 2)
+            def _():
+                a_copy(s, a, c, a_buf.at[s, a]).wait_recv()
             w[a, b] = w[a, b] - matmul(a_buf[s, a], xc[s])
 
     def update_row(s, a, b):
@@ -200,7 +202,27 @@
                 b_copy(s, a, b, r, b_buf.at[s, a, b]).wait_recv()
             w[a, b] = w[a, b] - matmul(xr[s, a], b_buf[s, a, b])
 
+    def direct_a(a):
+        return remote(a_in.at[a], a_buf.at[3, a], a_send.at[1, a], a_recv.at[3, a], r, col_next2)
+
+    def leave_a(go):
+        for a in range(2):
+            @pl.when((mod(shift, 8) == 2) & needs_a(3, r, col_next2, a))
+            def _(a=a):
+                go(direct_a(a))
+
+    def relay_a():
+        for a in range(2):
+            @pl.when(needs_a(3, r, col_next, a) & (mod(shift, 8) != 3))
+            def _(a=a):
+                a_copy(3, a, col_next, a_buf.at[2, a]).start()
+
     def hand_on():
+        for a in range(2):
+            @pl.when(needs_a(2, r, c, a))
+            def _(a=a):
+                a_copy(2, a, c, a_buf.at[2, a]).wait_recv()
+
         def one(a, b):
             @pl.when(needs_b(2, r, c, a, b))
             def _():
@@ -302,9 +324,7 @@
         when(0, lambda: send_b(0, row_next))
         when(jnp.where(h == 1, 1, 0), lambda: send_a(2, col_next))
         when(jnp.where((core == 0) & (h == 1), 1, 0), lambda: send_b(2, row_prev))
-        late = (core == 0) & (z > 1)
-        when(jnp.where(late, 2, jnp.where(h == 1, 1, jnp.where(h == 2, 2, 0))), lambda: send_a(3, col_next2, (0,)))
-        when(jnp.where(late, 3, jnp.where(h == 1, 1, jnp.where(h == 2, 2, 0))), lambda: send_a(3, col_next2, (1,)))
+        when(2, lambda: leave_a(lambda copy: copy.start()))
 
         @pl.when(core == 1)
         def _():
@@ -334,7 +354,7 @@
                     take(row_route(s, 1 - a, q))
                 each_piece(both)
 
-            pl.when((t == 3) & (turn == 3))(hand_on)
+            pl.when((t == 3) & (turn == 3) & (mod(shift, 8) == 3))(hand_on)
 
             @pl.when(ahead)
             def _():
@@ -351,7 +371,9 @@
             lax.fori_loop(0, t, catch_up, 0)
 
         stream(t)
-        pl.when((t == 3) & (turn != 3))(hand_on)
+        prompt = (mod(shift, 8) > 3) | (mod(shift, 8) < 2)
+        pl.when(jnp.where(prompt, t == 2, (t == 3) & (turn != 3)))(hand_on)
+        pl.when(jnp.where(prompt & ((z != 3) | (y != 0)), t == 2, t == 3))(relay_a)
 
         def rest(m, carry):
             p = jnp.where(t == FRONTS, jnp.where(m < 2, 2 * m, FRONTS - 1), 1)
@@ -387,11 +409,12 @@
     lax.fori_loop(0, 4, last, 0)
 
     def drain_a(a):
-        for s, col in ((0, col_prev), (2, col_next), (3, col_next2)):
-            @pl.when(needs_a(s, r, col, a))
+        for s, col in ((0, col_prev), (2, col_next), (3, col_next)):
+            @pl.when(needs_a(s, r, col, a) & ((mod(shift, 8) != 3) if s == 3 else True))
             def _(s=s, col=col):
                 a_copy(s, a, col, a_in.at[a]).wait_send()
     each_a(drain_a)
+    leave_a(lambda copy: copy.wait_send())
 
     def drain_b(a, b):
         for s, row in ((0, row_next), (2, row_prev)):

time: 131 us -> 124 us (0.947)
  the two profiles are of different devices: /device:TPU:76 before, /device:TPU:102 now
where the time goes in v4:
time: 124 us
  Pallas kernels  111 us (90%)
  local copies, waits for them, and re-layouts  13 us (10%)
    pallas_call x1, Pallas kernels, shards(): pl.pallas_call(functools.partial(plan, nb, n_row, n_col), out_shape=jax.S...  111 us
    unnamed x3, local copies, waits for them, and re-layouts  11.1 us

profile of v4, /device:TPU:102, one launch (start us, length us, event | category | flops | bytes accessed | tf_op | source)
XLA Modules:
  0.0 123.8 jit_solution(4443806579499896954)
XLA Ops:
  0.0 3.3 %copy.14 = bf16[2,512,2,512]{3,1,2,0:T(8,128)(2,1)} copy(bf16[2,512,2,512]{3,2,1,0:T(2,128)(2,1)} %param.9) | data formatting | bytes 4194304 | tf_op args[2]
  3.3 0.0 slice-start
  3.3 1.9 %slice-done = bf16[3,512,2,512]{3,2,1,0:T(2,128)(2,1)S(1)} async-done(((bf16[4,512,2,512]{3,2,1,0:T(2,128)(2,1)}), bf16[3,512,2,512]{3,2,1,0:T(2,128)(2,1)S(1)}, s32[]{:S(2)}) %slice-start) | async-done | bytes 3145752 | tf_op jit(solution)/shard_map/slice | solution.py:448
  5.1 2.2 %copy.13 = bf16[3,512,2,512]{3,1,2,0:T(8,128)(2,1)} copy(bf16[3,512,2,512]{3,2,1,0:T(2,128)(2,1)S(1)} %slice-done) | data formatting | bytes 6291456
  7.4 110.8 %shard_map.73 = f32[2,512,2,512]{3,2,1,0:T(2,128)} custom-call(bf16[2,512,512]{2,1,0:T(8,128)(2,1)} %a_in.1, bf16[3,2,512,512]{3,2,1,0:T(8,128)(2,1)} %bitcast.6, bf16[2,2,512,512]{3,2,1,0:T(8,128)(2,1)} %bitcast.7, bf16[2,512,512]{2,1,0:T(8,128)(2,1)} %qa_in.1, bf16[2,512,512]{2,1,0:T(8,128)(2,1)} %qb_in.1, f32[2,512]{1,0:T(2,128)} %av_in.1, f32[2,512]{1,0:T(2,128)} %bv_in.1), custom_call_target="tpu_custom_call" | custom-call | tf_op jit(solution)/shard_map/pallas_call | solution.py:451
  118.2 5.6 %copy.16 = f32[2,512,2,512]{3,2,1,0:T(2,128)} copy(f32[2,512,2,512]{3,2,1,0:T(2,128)} %shard_map.73) | data formatting | bytes 8388608
Async XLA Ops:
  3.3 1.9 %slice-start = ((bf16[4,512,2,512]{3,2,1,0:T(2,128)(2,1)}), bf16[3,512,2,512]{3,2,1,0:T(2,128)(2,1)S(1)}, s32[]{:S(2)}) async-start(bf16[4,512,2,512]{3,2,1,0:T(2,128)(2,1)} %param.8), calls=%async_computation | async-start | bytes 6291456 | tf_op jit(solution)/shard_map/slice | solution.py:448
